TPU v7x, 32 devices: a whole 2x2x4 slice. The times are simulated.
32 devices in a mesh: slab: 32 (over z, y, x, core).
Axes of the slice: x: 2, y: 2, z: 4, core: 2. Of those that a mesh axis runs over, the one named last changes fastest.
Arguments:
- load_terms: float32 [8, 8, 8, 4096], P(None, None, None, 'slab'), may hold values from -12 to 12
- geometry: float32 [3, 8, 8, 8, 4096], P(None, None, None, None, 'slab'), may hold values from 0.02 to 0.2
- mass_terms: float32 [8, 8, 8, 4096], P(None, None, None, 'slab'), may hold values from 1 to 4
- element_order: int32 [32, 128], P('slab'), may hold values from 0 to 127, each once within a row
Outputs:
- solution: float32 [8, 8, 8, 4096], P(None, None, None, 'slab')
- residual: float32 [8, 8, 8, 4096], P(None, None, None, 'slab')
Inputs may be any that keep to these rules, and one draw needn't show every extreme that they name: `element_order`: each device's row lists each of its 128 cells once.
All inputs are finite; a program needn't handle non-finite values.
Results may differ from a plain program's by a relative error of at most 0.0001.
Values sent between devices are 32-bit elements; how exact they have to be, the bound alone decides.
A program may use at most 64 MiB of HBM per device.

v0:
```python
import functools

import jax
import jax.numpy as jnp
import numpy as np
from jax import lax
from jax.experimental import pallas as pl
from jax.experimental.pallas import tpu as pltpu
from jax.sharding import PartitionSpec as P

EL_Y = 8
EL_Z = 16
MESH = pl.DeviceIdType.MESH
WIDEST = 32

spectrum_centre = 1.65
spectrum_half = 1.35


def legendre_table(positions, points):
    columns = [positions * 0.0 + 1.0, positions]
    for degree_now in range(2, points):
        columns.append(
            ((2 * degree_now - 1) * positions * columns[-1] - (degree_now - 1) * columns[-2])
            / degree_now
        )
    return np.stack(columns, axis=1)


def gll_derivative(points):
    degree = points - 1
    grid_nodes = -np.cos(np.pi * np.arange(points) / degree)
    for repeat in range(100):
        legendre = legendre_table(grid_nodes, points)
        grid_nodes = grid_nodes - (grid_nodes * legendre[:, degree] - legendre[:, degree - 1]) / (
            points * legendre[:, degree]
        )
    legendre = legendre_table(grid_nodes, points)
    top_values = legendre[:, degree]
    index_list = np.arange(points)
    same_index = index_list[:, None] == index_list[None, :]
    spacing = grid_nodes[:, None] - grid_nodes[None, :]
    spacing = np.where(same_index, 1.0, spacing)
    deriv_table = top_values[:, None] / (top_values[None, :] * spacing)
    deriv_table = np.where(same_index, 0.0, deriv_table)
    deriv_table[0, 0] = -degree * points / 4.0
    deriv_table[degree, degree] = degree * points / 4.0
    return deriv_table


def radices(count):
    factors = []
    while count > 1:
        width = max([w for w in range(2, WIDEST + 1) if count % w == 0], default=count)
        factors.append(width)
        count //= width
    return factors


def contract(values, table, symmetric):
    points = len(values)
    half = points // 2
    even = [values[j] + values[points - 1 - j] for j in range(half)]
    odd = [values[j] - values[points - 1 - j] for j in range(half)]
    low, high = [], []
    for m in range(half):
        a = [float(0.5 * (table[m, j] + table[m, points - 1 - j])) for j in range(half)]
        b = [float(0.5 * (table[m, j] - table[m, points - 1 - j])) for j in range(half)]
        part_even = a[0] * even[0]
        part_odd = b[0] * odd[0]
        for j in range(1, half):
            part_even = part_even + a[j] * even[j]
            part_odd = part_odd + b[j] * odd[j]
        low.append(part_even + part_odd)
        high.append(part_even - part_odd if symmetric else part_odd - part_even)
    return low + high[::-1]


def lane_gather(values, columns):
    dims = lax.GatherDimensionNumbers(
        offset_dims=(),
        collapsed_slice_dims=(1,),
        start_index_map=(1,),
        operand_batching_dims=(0,),
        start_indices_batching_dims=(0,),
    )
    return lax.gather(
        values, columns[..., None], dims, (1, 1), mode=lax.GatherScatterMode.PROMISE_IN_BOUNDS
    )


def kernel(
    count, points, factors, deriv,
    load_hbm, geo_hbm, mass_hbm, order_hbm, sol_ref, res_ref,
    load, geo, mass, start, inverse, vec, work, image,
    face_out, face_in, own_inv, near_inv, order, coef, sums, *rest,
):
    parts_in = rest[: len(factors)]
    (in_sem, face_send, face_recv, inv_sem, sum_send, sum_recv) = rest[len(factors):]
    me = lax.axis_index("slab")
    right = lax.rem(me + 1, count)
    left = lax.rem(me + count - 1, count)
    plane = points * points
    rows = points * plane
    last = rows - plane
    cols = load.shape[1]

    fetch = [
        pltpu.make_async_copy(geo_hbm, geo, in_sem.at[0]),
        pltpu.make_async_copy(mass_hbm, mass, in_sem.at[1]),
        pltpu.make_async_copy(load_hbm, load, in_sem.at[2]),
        pltpu.make_async_copy(order_hbm, order, in_sem.at[3]),
    ]
    for copy in fetch[::-1][:1] + fetch[:3]:
        copy.start()

    def peer(stride, width, k):
        digit = lax.rem(me // stride, width)
        return me + (lax.rem(digit + k, width) - digit) * stride

    strides = [int(np.prod(factors[:i])) for i in range(len(factors))]
    barrier = pltpu.get_barrier_semaphore()
    for near in (left, right):
        pl.semaphore_signal(barrier, inc=1, device_id=(near,), device_id_type=MESH)
    for stride, width in zip(strides, factors):
        @pl.loop(1, width)
        def _(k):
            pl.semaphore_signal(
                barrier, inc=1, device_id=(peer(stride, width, k),), device_id_type=MESH
            )

    fetch[3].wait()
    cell = order[...]
    cell8 = jnp.broadcast_to(cell, (points, cols))
    cell_col = jnp.transpose(jnp.broadcast_to(cell.astype(jnp.float32), (cols, cols)))
    lane = lax.broadcasted_iota(jnp.int32, (cols, cols), 1).astype(jnp.float32)
    source = lax.broadcasted_iota(jnp.int32, (cols, cols), 0).astype(jnp.float32)
    inv_row = jnp.sum(jnp.where(cell_col == lane, source, 0.0), axis=0, keepdims=True)
    inv8 = jnp.broadcast_to(inv_row.astype(jnp.int32), (points, cols))
    own_inv[...] = inv8
    pos_z = cell8 % EL_Z
    has_up = cell8 < cols - EL_Z
    has_down = cell8 >= EL_Z
    plus_y = lane_gather(inv8, jnp.where(has_up, cell8 + EL_Z, cell8))
    minus_y = lane_gather(inv8, jnp.where(has_down, cell8 - EL_Z, cell8))
    plus_z = lane_gather(inv8, jnp.where(pos_z == EL_Z - 1, cell8 - (EL_Z - 1), cell8 + 1))
    minus_z = lane_gather(inv8, jnp.where(pos_z == 0, cell8 + (EL_Z - 1), cell8 - 1))

    row_id = lax.broadcasted_iota(jnp.int32, (points, cols), 0)
    for t, table in enumerate((deriv, deriv.T, (deriv * deriv).T)):
        for k in range(points):
            vector = jnp.zeros((points, cols), jnp.float32)
            for m in range(points):
                vector = jnp.where(row_id == m, float(table[m, (m - k) % points]), vector)
            coef[t, k] = vector

    def rotate_contract(value, t):
        total = coef[t, 0] * value
        for k in range(1, points):
            total = total + coef[t, k] * pltpu.roll(value, k, 0)
        return total

    def send_pair(low_src, high_src, dst, send_sem, recv_sem):
        for src, side, near in ((low_src, 1, left), (high_src, 0, right)):
            pltpu.make_async_remote_copy(
                src_ref=src, dst_ref=dst.at[side], send_sem=send_sem, recv_sem=recv_sem,
                device_id=(near,), device_id_type=MESH,
            ).start()

    def settle(ref, send_sem, recv_sem):
        return pltpu.make_async_remote_copy(
            src_ref=ref, dst_ref=ref, send_sem=send_sem, recv_sem=recv_sem,
            device_id=(right,), device_id_type=MESH,
        )

    def send_faces(e):
        send_pair(face_out.at[e, 0], face_out.at[e, 1], face_in.at[e], face_send, face_recv.at[e])

    def wait_faces(e):
        settle(face_in.at[e], face_send, face_recv.at[e]).wait_recv()

    def at(base, b):
        return pl.ds(base + b * points, points)

    def geo_at(k, base, b):
        return pl.ds(k * rows + base + b * points, points)

    def store_face(e, side, b, value):
        face_out[e, side, pl.ds(b * points, points)] = value

    inner = [a * plane for a in range(1, points - 1)]

    def assemble_planes(spots):
        lows = [ref[at(base, 0)] for ref, base in spots]
        highs = [ref[at(base, points - 1)] for ref, base in spots]
        from_low = [lane_gather(low, plus_y) for low in lows]
        from_high = [lane_gather(high, minus_y) for high in highs]
        for i, (ref, base) in enumerate(spots):
            ref[at(base, points - 1)] = highs[i] + jnp.where(has_up, from_low[i], 0.0)
            ref[at(base, 0)] = lows[i] + jnp.where(has_down, from_high[i], 0.0)
        firsts = [pl.ds(base, points, stride=points) for _, base in spots]
        ends = [pl.ds(base + points - 1, points, stride=points) for _, base in spots]
        lows = [ref[first] for (ref, _), first in zip(spots, firsts)]
        highs = [ref[end] for (ref, _), end in zip(spots, ends)]
        from_low = [lane_gather(low, plus_z) for low in lows]
        from_high = [lane_gather(high, minus_z) for high in highs]
        for i, (ref, _) in enumerate(spots):
            ref[ends[i]] = highs[i] + from_low[i]
            ref[firsts[i]] = lows[i] + from_high[i]

    square = deriv * deriv
    fetch[0].wait()
    fetch[1].wait()

    for b in range(points):
        values = [geo[geo_at(0, a * plane, b)] for a in range(points)]
        for a, value in enumerate(contract(values, square.T, True)):
            work[at(a * plane, b)] = value

    def diagonal_plane(base, put):
        values = [geo[geo_at(1, base, b)] for b in range(points)]
        for b, value in enumerate(contract(values, square.T, True)):
            value = value + rotate_contract(geo[geo_at(2, base, b)], 2)
            put(b, value + work[at(base, b)] + mass[at(base, b)])

    diagonal_plane(0, functools.partial(store_face, 1, 0))
    diagonal_plane(last, functools.partial(store_face, 1, 1))
    pl.semaphore_wait(barrier, 2 + sum(w - 1 for w in factors))
    send_pair(
        load_hbm.at[pl.ds(0, plane)], load_hbm.at[pl.ds(last, plane)],
        face_in.at[0], face_send, face_recv.at[0],
    )
    send_pair(own_inv, own_inv, near_inv, inv_sem.at[0], inv_sem.at[1])
    send_faces(1)

    def first_update(base):
        for b in range(points):
            span = at(base, b)
            scaled = 1.0 / inverse[span]
            inverse[span] = scaled
            vec[span] = scaled * start[span] * (1.0 / spectrum_centre)

    fetch[2].wait()

    for base in inner:
        for b in range(points):
            start[at(base, b)] = load[at(base, b)]
    assemble_planes([(start, base) for base in inner])
    for base in inner:

        def put(b, value):
            inverse[at(base, b)] = value

        diagonal_plane(base, put)
    assemble_planes([(inverse, base) for base in inner])
    for base in inner:
        first_update(base)

    def along_first(put):
        for b in range(points):
            values = [vec[at(a * plane, b)] for a in range(points)]
            slopes = contract(values, deriv, False)
            fluxes = [geo[geo_at(0, a * plane, b)] * slopes[a] for a in range(points)]
            for a, value in enumerate(contract(fluxes, deriv.T, False)):
                put(a, b, value)

    def in_plane(base, ref):
        values = [vec[at(base, b)] for b in range(points)]
        slopes = contract(values, deriv, False)
        fluxes = [geo[geo_at(1, base, b)] * slopes[b] for b in range(points)]
        for b, value in enumerate(contract(fluxes, deriv.T, False)):
            flux = geo[geo_at(2, base, b)] * rotate_contract(values[b], 0)
            value = value + rotate_contract(flux, 1)
            ref[at(base, b)] = value + mass[at(base, b)] * values[b]

    def apply_faces_first(e, extra):
        for base in (0, last):
            in_plane(base, work)

        def put(a, b, term):
            span = at(a * plane, b)
            if a in (0, points - 1):
                out = work[span] + term
                store_face(e, int(a > 0), b, out)
            else:
                out = image[span] + term
                image[span] = out
            extra(span, out)

        along_first(put)
        send_faces(e)

    for base in inner:
        in_plane(base, image)

    settle(near_inv, inv_sem.at[0], inv_sem.at[1]).wait()
    minus_x = lane_gather(near_inv[0], cell8)
    plus_x = lane_gather(near_inv[1], cell8)

    def join_faces(e, own, ref):
        for side, (base, columns) in enumerate(((0, minus_x), (last, plus_x))):
            for b in range(points):
                ref[at(base, b)] = own(side, b) + lane_gather(
                    face_in[e, side, pl.ds(b * points, points)], columns
                )
        assemble_planes([(ref, 0), (ref, last)])

    def own_face(e):
        return lambda side, b: face_out[e, side, pl.ds(b * points, points)]

    wait_faces(0)
    join_faces(0, lambda side, b: load[at((0, last)[side], b)], start)
    wait_faces(1)
    join_faces(1, own_face(1), inverse)
    first_update(0)
    first_update(last)

    ratio_sigma = spectrum_centre / spectrum_half
    rho_prev = 1.0 / ratio_sigma
    rho_next = 1.0 / (2.0 * ratio_sigma - rho_prev)
    on_misfit = 2.0 * rho_next / spectrum_half
    on_start = (1.0 + rho_next * rho_prev) / spectrum_centre + on_misfit

    def second_update(base):
        for b in range(points):
            span = at(base, b)
            vec[span] = inverse[span] * (on_start * start[span] - on_misfit * image[span])

    apply_faces_first(2, lambda span, out: None)
    assemble_planes([(image, base) for base in inner])
    for base in inner:
        second_update(base)

    def sum_of(terms):
        while len(terms) > 1:
            terms = [x + y for x, y in zip(terms[::2], terms[1::2])] + terms[len(terms) & ~1:]
        return terms[0]

    def load_product(base):
        return sum_of([load[at(base, b)] * vec[at(base, b)] for b in range(points)])

    for base in inner:
        in_plane(base, image)
    on_load = sum_of([load_product(base) for base in inner])

    wait_faces(2)
    join_faces(2, own_face(2), image)
    second_update(0)
    second_update(last)

    products = []
    apply_faces_first(3, lambda span, out: products.append(vec[span] * out))
    on_load = on_load + load_product(0) + load_product(last)
    tally = [on_load, sum_of(products)]
    total = jnp.concatenate([jnp.sum(part, axis=0, keepdims=True) for part in tally], axis=1)

    def sum_copy(i, k):
        stride, width = strides[i], factors[i]
        return pltpu.make_async_remote_copy(
            src_ref=sums.at[i], dst_ref=parts_in[i].at[k - 1],
            send_sem=sum_send.at[i], recv_sem=sum_recv.at[i],
            device_id=(peer(stride, width, k),), device_id_type=MESH,
        )

    def start_sum(i, value):
        sums[i] = value

        @pl.loop(1, factors[i])
        def _(k):
            sum_copy(i, k).start()

    def finish_sum(i, value):
        settle(parts_in[i], sum_send.at[i], sum_recv.at[i]).wait()
        for k in range(factors[i] - 1):
            value = value + parts_in[i][k]
        return value

    start_sum(0, total)

    assemble_planes([(image, base) for base in inner])

    wait_faces(3)
    join_faces(3, own_face(3), image)
    for i in range(len(factors)):
        if i:
            start_sum(i, total)
        total = finish_sum(i, total)
    settle(face_out, face_send, face_recv.at[0]).wait_send()
    numerator = jnp.sum(total[:, :cols], axis=1, keepdims=True)
    denominator = jnp.sum(total[:, cols:], axis=1, keepdims=True)
    size = jnp.broadcast_to(numerator / denominator, (points, cols))

    for a in range(points):
        for b in range(points):
            span = at(a * plane, b)
            sol_ref[span] = size * vec[span]
            res_ref[span] = start[span] - size * image[span]


def on_device(count, load_terms, geometry, mass_terms, element_order):
    points = load_terms.shape[0]
    cols = load_terms.shape[3]
    plane = points * points
    rows = points * plane
    deriv = gll_derivative(points)
    factors = radices(count)
    f32 = jnp.float32
    big = [pltpu.VMEM((rows, cols), f32)]
    scratch = (
        big + [pltpu.VMEM((3 * rows, cols), f32)] + big * 6
        + [
            pltpu.VMEM((4, 2, plane, cols), f32),
            pltpu.VMEM((4, 2, plane, cols), f32),
            pltpu.VMEM((points, cols), jnp.int32),
            pltpu.VMEM((2, points, cols), jnp.int32),
            pltpu.VMEM((1, cols), jnp.int32),
            pltpu.VMEM((3, points, points, cols), f32),
            pltpu.VMEM((len(factors), 1, 2 * cols), f32),
        ]
        + [pltpu.VMEM((w - 1, 1, 2 * cols), f32) for w in factors]
        + [
            pltpu.SemaphoreType.DMA((4,)),
            pltpu.SemaphoreType.DMA,
            pltpu.SemaphoreType.DMA((4,)),
            pltpu.SemaphoreType.DMA((2,)),
            pltpu.SemaphoreType.DMA((len(factors),)),
            pltpu.SemaphoreType.DMA((len(factors),)),
        ]
    )
    hbm = pl.BlockSpec(memory_space=pl.ANY)
    vmem = pl.BlockSpec(memory_space=pltpu.VMEM)
    solution_rows, residual_rows = pl.pallas_call(
        functools.partial(kernel, count, points, factors, deriv),
        out_shape=(pltpu.VMEM((rows, cols), f32),) * 2,
        in_specs=[hbm] * 4,
        out_specs=(vmem, vmem),
        scratch_shapes=scratch,
        compiler_params=pltpu.CompilerParams(collective_id=0, has_side_effects=True),
    )(
        load_terms.reshape(rows, cols),
        geometry.reshape(3 * rows, cols),
        mass_terms.reshape(rows, cols),
        element_order,
    )
    shape = load_terms.shape
    return solution_rows.reshape(shape), residual_rows.reshape(shape)


def solution(mesh):
    placed = (
        P(None, None, None, "slab"),
        P(None, None, None, None, "slab"),
        P(None, None, None, "slab"),
        P("slab", None),
    )
    return jax.shard_map(
        functools.partial(on_device, mesh.shape["slab"]),
        mesh=mesh,
        in_specs=placed,
        out_specs=(P(None, None, None, "slab"), P(None, None, None, "slab")),
        check_vma=False,
    )
```

profile of v0, /device:TPU:0, one launch (start us, length us, event | category | flops | bytes accessed | tf_op | source)
XLA Modules:
  0.0 22.3 jit_solution(16661349491252742893)
XLA Ops:
  0.6 20.2 %shard_map.59 = (f32[512,128]{1,0:T(8,128)S(1)}, f32[512,128]{1,0:T(8,128)S(1)}) custom-call(f32[512,128]{1,0:T(8,128)} %bitcast.8, f32[1536,128]{1,0:T(8,128)} %bitcast.7, f32[512,128]{1,0:T(8,128)} %bitcast.9, s32[1,128]{1,0:T(1,128)} %order_hbm.1), custom_call_target="tpu_custom_call" | custom-call | tf_op jit(solution)/shard_map/pallas_call | solution.py:432
  20.9 0.7 %copy.8 = f32[8,8,8,128]{3,2,1,0:T(8,128)} copy(f32[8,8,8,128]{3,2,1,0:T(8,128)S(1)} %bitcast.6) | data formatting | bytes 524288
  21.6 0.7 %copy.9 = f32[8,8,8,128]{3,2,1,0:T(8,128)} copy(f32[8,8,8,128]{3,2,1,0:T(8,128)S(1)} %bitcast.5) | data formatting | bytes 524288
where the time goes:
time: 22.4 us; the launch traced here: 22.3 us
  Pallas kernels  20.2 us (90%)
  local copies, waits for them, and re-layouts  1.41 us (6%)
  between operations  0.64 us (3%)
    pallas_call x1, Pallas kernels, on_device(): pl.pallas_call(functools.partial(kernel, count, points, factors, deriv),...  20.2 us
    unnamed x2, local copies, waits for them, and re-layouts  1.41 us

commit v1 on v0

v1 whole, which is shorter than its diff:
```python
import functools

import jax
import jax.numpy as jnp
import numpy as np
from jax import lax
from jax.experimental import pallas as pl
from jax.experimental.pallas import tpu as pltpu
from jax.sharding import PartitionSpec as P

EL_Y = 8
EL_Z = 16
MESH = pl.DeviceIdType.MESH
WIDEST = 32

spectrum_centre = 1.65
spectrum_half = 1.35


def legendre_table(positions, points):
    columns = [positions * 0.0 + 1.0, positions]
    for degree_now in range(2, points):
        columns.append(
            ((2 * degree_now - 1) * positions * columns[-1] - (degree_now - 1) * columns[-2])
            / degree_now
        )
    return np.stack(columns, axis=1)


def gll_derivative(points):
    degree = points - 1
    grid_nodes = -np.cos(np.pi * np.arange(points) / degree)
    for repeat in range(100):
        legendre = legendre_table(grid_nodes, points)
        grid_nodes = grid_nodes - (grid_nodes * legendre[:, degree] - legendre[:, degree - 1]) / (
            points * legendre[:, degree]
        )
    legendre = legendre_table(grid_nodes, points)
    top_values = legendre[:, degree]
    index_list = np.arange(points)
    same_index = index_list[:, None] == index_list[None, :]
    spacing = grid_nodes[:, None] - grid_nodes[None, :]
    spacing = np.where(same_index, 1.0, spacing)
    deriv_table = top_values[:, None] / (top_values[None, :] * spacing)
    deriv_table = np.where(same_index, 0.0, deriv_table)
    deriv_table[0, 0] = -degree * points / 4.0
    deriv_table[degree, degree] = degree * points / 4.0
    return deriv_table


def radices(count):
    factors = []
    while count > 1:
        width = max([w for w in range(2, WIDEST + 1) if count % w == 0], default=count)
        factors.append(width)
        count //= width
    return factors


def contract(values, table, symmetric, skip_in=0, skip_out=0):
    points = len(values)
    half = points // 2
    ins = range(skip_in, half)
    even = {j: values[j] + values[points - 1 - j] for j in ins}
    odd = {j: values[j] - values[points - 1 - j] for j in ins}
    low, high = [], []
    for m in range(skip_out, half):
        part_even, part_odd = None, None
        for j in ins:
            a = float(0.5 * (table[m, j] + table[m, points - 1 - j]))
            b = float(0.5 * (table[m, j] - table[m, points - 1 - j]))
            part_even = a * even[j] if part_even is None else part_even + a * even[j]
            part_odd = b * odd[j] if part_odd is None else part_odd + b * odd[j]
        low.append(part_even + part_odd)
        high.append(part_even - part_odd if symmetric else part_odd - part_even)
    return low + high[::-1]


def end_columns(values, deriv):
    points = len(values)
    half = points // 2
    even = [values[m] + values[points - 1 - m] for m in range(half)]
    odd = [values[m] - values[points - 1 - m] for m in range(half)]
    low, high = {}, {}
    for a in range(1, points - 1):
        product = deriv[:, 0] * deriv[:, a]
        part_even, part_odd = None, None
        for m in range(half):
            p = float(0.5 * (product[m] + product[points - 1 - m]))
            q = float(0.5 * (product[m] - product[points - 1 - m]))
            part_even = p * even[m] if part_even is None else part_even + p * even[m]
            part_odd = q * odd[m] if part_odd is None else part_odd + q * odd[m]
        low[a] = part_even + part_odd
        high[points - 1 - a] = part_even - part_odd
    product = deriv[:, 0] * deriv[:, points - 1]
    cross = float(product[0]) * even[0]
    for m in range(1, half):
        cross = cross + float(product[m]) * even[m]
    return low, high, cross


def sum_of(terms):
    while len(terms) > 1:
        terms = [x + y for x, y in zip(terms[::2], terms[1::2])] + terms[len(terms) & ~1:]
    return terms[0]


def lane_gather(values, columns):
    dims = lax.GatherDimensionNumbers(
        offset_dims=(),
        collapsed_slice_dims=(1,),
        start_index_map=(1,),
        operand_batching_dims=(0,),
        start_indices_batching_dims=(0,),
    )
    return lax.gather(
        values, columns[..., None], dims, (1, 1), mode=lax.GatherScatterMode.PROMISE_IN_BOUNDS
    )


def kernel(
    count, points, factors, deriv,
    load_hbm, geo_hbm, mass_hbm, order_hbm, start, vec, image, size_ref,
    load, geo, mass, inverse, work,
    first_out, first_in, pair_in, pair, pair_diag, face_diag,
    ends, cross, inner_part, along_out, along_in,
    own_inv, near_inv, across, order, coef, sums, *rest,
):
    parts_in = rest[: len(factors)]
    (
        in_sem, first_send, first_recv, inv_send, inv_recv, pair_send, pair_recv,
        along_send, along_recv, sum_send, sum_recv,
    ) = rest[len(factors):]
    me = lax.axis_index("slab")
    right = lax.rem(me + 1, count)
    left = lax.rem(me + count - 1, count)
    plane = points * points
    rows = points * plane
    last = rows - plane
    cols = load.shape[1]
    odd_one = lax.rem(me, 2)
    near = 1 - odd_one
    far = odd_one
    near_device = lax.rem(me + count + 1 - 2 * odd_one, count)
    far_device = lax.rem(me + count - 1 + 2 * odd_one, count)
    device_of = ((far, far_device), (near, near_device))

    fetch = [
        pltpu.make_async_copy(geo_hbm, geo, in_sem.at[0]),
        pltpu.make_async_copy(mass_hbm, mass, in_sem.at[1]),
        pltpu.make_async_copy(load_hbm, load, in_sem.at[2]),
        pltpu.make_async_copy(order_hbm, order, in_sem.at[3]),
    ]
    for copy in fetch[::-1][:1] + fetch[:3]:
        copy.start()

    def peer(stride, width, k):
        digit = lax.rem(me // stride, width)
        return me + (lax.rem(digit + k, width) - digit) * stride

    strides = [int(np.prod(factors[:i])) for i in range(len(factors))]
    barrier = pltpu.get_barrier_semaphore()
    for beside in (left, right):
        pl.semaphore_signal(barrier, inc=1, device_id=(beside,), device_id_type=MESH)
    for stride, width in zip(strides, factors):
        @pl.loop(1, width)
        def _(k):
            pl.semaphore_signal(
                barrier, inc=1, device_id=(peer(stride, width, k),), device_id_type=MESH
            )

    fetch[3].wait()
    cell = order[...]
    cell8 = jnp.broadcast_to(cell, (points, cols))
    cell_col = jnp.transpose(jnp.broadcast_to(cell.astype(jnp.float32), (cols, cols)))
    lane = lax.broadcasted_iota(jnp.int32, (cols, cols), 1).astype(jnp.float32)
    source = lax.broadcasted_iota(jnp.int32, (cols, cols), 0).astype(jnp.float32)
    inv_row = jnp.sum(jnp.where(cell_col == lane, source, 0.0), axis=0, keepdims=True)
    inv8 = jnp.broadcast_to(inv_row.astype(jnp.int32), (points, cols))
    own_inv[...] = inv8
    pos_z = cell8 % EL_Z
    has_up = cell8 < cols - EL_Z
    has_down = cell8 >= EL_Z
    plus_y = lane_gather(inv8, jnp.where(has_up, cell8 + EL_Z, cell8))
    minus_y = lane_gather(inv8, jnp.where(has_down, cell8 - EL_Z, cell8))
    plus_z = lane_gather(inv8, jnp.where(pos_z == EL_Z - 1, cell8 - (EL_Z - 1), cell8 + 1))
    minus_z = lane_gather(inv8, jnp.where(pos_z == 0, cell8 + (EL_Z - 1), cell8 - 1))

    row_id = lax.broadcasted_iota(jnp.int32, (points, cols), 0)
    for t, table in enumerate((deriv, deriv.T, (deriv * deriv).T)):
        for k in range(points):
            vector = jnp.zeros((points, cols), jnp.float32)
            for m in range(points):
                vector = jnp.where(row_id == m, float(table[m, (m - k) % points]), vector)
            coef[t, k] = vector
    share_z = jnp.where((row_id == 0) | (row_id == points - 1), 0.5, 1.0)
    share_low = jnp.where(has_down, 0.5 * share_z, share_z)
    share_high = jnp.where(has_up, 0.5 * share_z, share_z)

    def share(b):
        return share_low if b == 0 else share_high if b == points - 1 else share_z

    def rotate_contract(value, t):
        total = coef[t, 0] * value
        for k in range(1, points):
            total = total + coef[t, k] * pltpu.roll(value, k, 0)
        return total

    def post(src, dst, send_sem, recv_sem, device):
        pltpu.make_async_remote_copy(
            src_ref=src, dst_ref=dst, send_sem=send_sem, recv_sem=recv_sem,
            device_id=(device,), device_id_type=MESH,
        ).start()

    def settle(ref, send_sem, recv_sem):
        return pltpu.make_async_remote_copy(
            src_ref=ref, dst_ref=ref, send_sem=send_sem, recv_sem=recv_sem,
            device_id=(right,), device_id_type=MESH,
        )

    def line(b):
        return pl.ds(b * points, points)

    def at(base, b):
        if isinstance(base, int):
            return pl.ds(base + b * points, points)
        return pl.ds(pl.multiple_of(base + b * points, points), points)

    def geo_at(k, base, b):
        return at(k * rows + base, b)

    def end_base(s):
        return pl.multiple_of(s * last, points)

    inner = [a * plane for a in range(1, points - 1)]

    def assemble_planes(spots):
        lows = [ref[at(base, 0)] for ref, base in spots]
        highs = [ref[at(base, points - 1)] for ref, base in spots]
        from_low = [lane_gather(low, plus_y) for low in lows]
        from_high = [lane_gather(high, minus_y) for high in highs]
        for i, (ref, base) in enumerate(spots):
            ref[at(base, points - 1)] = highs[i] + jnp.where(has_up, from_low[i], 0.0)
            ref[at(base, 0)] = lows[i] + jnp.where(has_down, from_high[i], 0.0)
        firsts = [pl.ds(base, points, stride=points) for _, base in spots]
        ends_at = [pl.ds(base + points - 1, points, stride=points) for _, base in spots]
        lows = [ref[first] for (ref, _), first in zip(spots, firsts)]
        highs = [ref[end] for (ref, _), end in zip(spots, ends_at)]
        from_low = [lane_gather(low, plus_z) for low in lows]
        from_high = [lane_gather(high, minus_z) for high in highs]
        for i, (ref, _) in enumerate(spots):
            ref[ends_at[i]] = highs[i] + from_low[i]
            ref[firsts[i]] = lows[i] + from_high[i]

    square = deriv * deriv
    fetch[0].wait()
    fetch[1].wait()

    for b in range(points):
        values = [geo[geo_at(0, a * plane, b)] for a in range(points)]
        for a, value in enumerate(contract(values, square.T, True)):
            work[at(a * plane, b)] = value

    def diagonal_plane(base, put):
        values = [geo[geo_at(1, base, b)] for b in range(points)]
        for b, value in enumerate(contract(values, square.T, True)):
            value = value + rotate_contract(geo[geo_at(2, base, b)], 2)
            put(b, value + work[at(base, b)] + mass[at(base, b)])

    for s, base in ((0, 0), (1, last)):

        def put(b, value):
            first_out[s, at(plane, b)] = value

        diagonal_plane(base, put)
    fetch[2].wait()
    for s, base in ((0, 0), (1, last)):
        for b in range(points):
            first_out[s, line(b)] = load[at(base, b)]
    assemble_planes([(first_out.at[s], k * plane) for s in (0, 1) for k in (0, 1)])

    for base in inner:
        for b in range(points):
            start[at(base, b)] = load[at(base, b)]

        def put(b, value):
            inverse[at(base, b)] = value

        diagonal_plane(base, put)
    assemble_planes([(ref, base) for base in inner for ref in (start, inverse)])
    for base in inner:
        for b in range(points):
            span = at(base, b)
            scaled = 1.0 / inverse[span]
            inverse[span] = scaled
            vec[span] = scaled * start[span] * (1.0 / spectrum_centre)
    for b in range(points):
        values = [geo[geo_at(0, a * plane, b)] for a in range(points)]
        low, high, both = end_columns(values, deriv)
        for a in range(1, points - 1):
            ends[0, at((a - 1) * plane, b)] = low[a]
            ends[1, at((a - 1) * plane, b)] = high[a]
        cross[line(b)] = both
    assemble_planes(
        [(ends.at[s], base - plane) for s in (0, 1) for base in inner] + [(cross, 0)]
    )

    def inner_to_ends():
        for b in range(points):
            values = [vec[at(base, b)] for base in inner]
            for s in (0, 1):
                inner_part[s, line(b)] = sum_of(
                    [ends[s, at(base - plane, b)] * v for base, v in zip(inner, values)]
                )

    inner_to_ends()

    pl.semaphore_wait(barrier, 2 + sum(w - 1 for w in factors))
    for s, device in device_of:
        post(first_out.at[s], first_in.at[1 - s], first_send, first_recv.at[1 - s], device)
        post(own_inv, near_inv.at[1 - s], inv_send, inv_recv.at[1 - s], device)
    for s, device in device_of:
        for k in (1, 2):
            post(
                geo.at[pl.ds(pl.multiple_of(k * rows + s * last, points), plane)],
                pair_in.at[1 - s, k - 1], pair_send, pair_recv.at[1 - s], device,
            )

    def in_plane(values, slope_geo, flux_geo):
        slopes = contract(values, deriv, False)
        fluxes = [slope_geo(b) * slopes[b] for b in range(points)]
        out = contract(fluxes, deriv.T, False)
        for b in range(points):
            flux = flux_geo(b) * rotate_contract(values[b], 0)
            out[b] = out[b] + rotate_contract(flux, 1)
        return out

    def apply_inner(extra):
        for b in range(points):
            values = [None] + [vec[at(base, b)] for base in inner] + [None]
            slopes = contract(values, deriv, False, skip_in=1)
            fluxes = [geo[geo_at(0, a * plane, b)] * slopes[a] for a in range(points)]
            terms = contract(fluxes, deriv.T, False, skip_out=1)
            for base, value in zip(inner, terms):
                work[at(base, b)] = value
        for base in inner:
            values = [vec[at(base, b)] for b in range(points)]
            terms = in_plane(
                values,
                lambda b: geo[geo_at(1, base, b)],
                lambda b: geo[geo_at(2, base, b)],
            )
            for b in range(points):
                span = at(base, b)
                out = terms[b] + work[span] + mass[span] * values[b]
                image[span] = out
                extra(span, values[b], out)

    apply_inner(lambda span, value, out: None)
    assemble_planes([(image, base) for base in inner])

    def meet(s):
        settle(near_inv.at[s], inv_send, inv_recv.at[s]).wait_recv()
        columns = lane_gather(near_inv[s], cell8)
        across[s] = columns
        settle(first_in.at[s], first_send, first_recv.at[s]).wait_recv()
        base = end_base(s)
        for b in range(points):
            span = at(base, b)
            begin = first_out[s, line(b)] + lane_gather(first_in[s, line(b)], columns)
            whole = first_out[s, at(plane, b)] + lane_gather(first_in[s, at(plane, b)], columns)
            scaled = 1.0 / whole
            face_diag[s, line(b)] = whole
            start[span] = begin
            inverse[span] = scaled
            vec[span] = scaled * begin * (1.0 / spectrum_centre)

    def send_along(e, s, other, device):
        base = end_base(other)
        for b in range(points):
            along_out[e, s, line(b)] = inner_part[s, line(b)] + cross[line(b)] * vec[at(base, b)]
        post(
            along_out.at[e, s], along_in.at[e, 1 - s], along_send.at[e],
            along_recv.at[e, 1 - s], device,
        )

    def join_pair(s):
        settle(pair_in.at[s], pair_send, pair_recv.at[s]).wait_recv()
        columns = across[s]
        for k in (0, 1):
            for b in range(points):
                own = geo[geo_at(k + 1, s * last, b)]
                pair[s, k, line(b)] = own + lane_gather(pair_in[s, k, line(b)], columns)
        terms = contract([pair[s, 0, line(b)] for b in range(points)], square.T, True)
        for b in range(points):
            pair_diag[s, line(b)] = terms[b] + rotate_contract(pair[s, 1, line(b)], 2)

    def apply_end(s, ref):
        base = end_base(s)
        values = [vec[at(base, b)] for b in range(points)]
        terms = in_plane(values, lambda b: pair[s, 0, line(b)], lambda b: pair[s, 1, line(b)])
        for b in range(points):
            terms[b] = terms[b] - pair_diag[s, line(b)] * values[b]
            ref[at(base, b)] = terms[b]
        return values, terms

    def first_end(s):
        apply_end(s, image)
        assemble_planes([(image, end_base(s))])

    ratio_sigma = spectrum_centre / spectrum_half
    rho_prev = 1.0 / ratio_sigma
    rho_next = 1.0 / (2.0 * ratio_sigma - rho_prev)
    on_misfit = 2.0 * rho_next / spectrum_half
    on_start = (1.0 + rho_next * rho_prev) / spectrum_centre + on_misfit

    def add_ends(base, b):
        return (
            image[at(base, b)]
            + ends[0, at(base - plane, b)] * vec[at(0, b)]
            + ends[1, at(base - plane, b)] * vec[at(last, b)]
        )

    def join_along(e, s, columns, b):
        span = at(end_base(s), b)
        return (
            image[span] + face_diag[s, line(b)] * vec[span] + along_out[e, s, line(b)]
            + lane_gather(along_in[e, s, line(b)], columns)
        )

    def second_end(s):
        settle(along_in.at[0, s], along_send.at[0], along_recv.at[0, s]).wait_recv()
        columns = across[s]
        for b in range(points):
            span = at(end_base(s), b)
            total = join_along(0, s, columns, b)
            vec[span] = inverse[span] * (on_start * start[span] - on_misfit * total)

    on_load, products = [], []

    def end_terms(s):
        values, terms = apply_end(s, image)
        for b in range(points):
            value = values[b]
            halved = 0.5 * value
            weighted = share(b) * value
            span = at(end_base(s), b)
            on_load.append(0.5 * weighted * start[span])
            products.append(
                halved * terms[b]
                + weighted * (face_diag[s, line(b)] * halved + 2.0 * inner_part[s, line(b)])
            )

    meet(near)
    send_along(0, far, near, far_device)
    join_pair(near)
    first_end(near)
    meet(far)
    send_along(0, near, far, near_device)
    for base in inner:
        for b in range(points):
            span = at(base, b)
            total = add_ends(base, b)
            vec[span] = inverse[span] * (on_start * start[span] - on_misfit * total)
    join_pair(far)
    first_end(far)
    inner_to_ends()
    second_end(near)
    send_along(1, far, near, far_device)

    def tally(span, value, out):
        products.append(value * out)
        on_load.append(load[span] * value)

    apply_inner(tally)
    end_terms(near)
    second_end(far)
    send_along(1, near, far, near_device)
    end_terms(far)
    for b in range(points):
        products.append(
            2.0 * share(b) * cross[line(b)] * vec[at(0, b)] * vec[at(last, b)]
        )
    total = jnp.concatenate(
        [jnp.sum(sum_of(part), axis=0, keepdims=True) for part in (on_load, products)], axis=1
    )

    def sum_copy(i, k):
        stride, width = strides[i], factors[i]
        return pltpu.make_async_remote_copy(
            src_ref=sums.at[i], dst_ref=parts_in[i].at[k - 1],
            send_sem=sum_send.at[i], recv_sem=sum_recv.at[i],
            device_id=(peer(stride, width, k),), device_id_type=MESH,
        )

    def start_sum(i, value):
        sums[i] = value

        @pl.loop(1, factors[i])
        def _(k):
            sum_copy(i, k).start()

    def finish_sum(i, value):
        settle(parts_in[i], sum_send.at[i], sum_recv.at[i]).wait()
        for k in range(factors[i] - 1):
            value = value + parts_in[i][k]
        return value

    start_sum(0, total)

    assemble_planes([(image, base) for base in [0] + inner + [last]])
    for base in inner:
        for b in range(points):
            image[at(base, b)] = add_ends(base, b)
    for s in (near, far):
        settle(along_in.at[1, s], along_send.at[1], along_recv.at[1, s]).wait_recv()
        columns = across[s]
        for b in range(points):
            image[at(end_base(s), b)] = join_along(1, s, columns, b)
    settle(first_out, first_send, first_recv.at[0]).wait_send()
    settle(near_inv, inv_send, inv_recv.at[0]).wait_send()
    settle(pair_in, pair_send, pair_recv.at[0]).wait_send()
    for e in (0, 1):
        settle(along_out.at[e], along_send.at[e], along_recv.at[0, 0]).wait_send()
    for i in range(len(factors)):
        if i:
            start_sum(i, total)
        total = finish_sum(i, total)
    numerator = jnp.sum(total[:, :cols], axis=1, keepdims=True)
    denominator = jnp.sum(total[:, cols:], axis=1, keepdims=True)
    size_ref[...] = jnp.broadcast_to(numerator / denominator, (points, cols))


def finish(pieces, points, start, vec, image, size, sol_hbm, res_hbm, sol, res, sems):
    rows, cols = start.shape
    scale = size[...]
    step = rows // pieces
    copies = []
    for i in range(pieces):
        part = pl.ds(i * step, step)
        for j in range(step // points):
            span = pl.ds(i * step + j * points, points)
            sol[span] = scale * vec[span]
            res[span] = start[span] - scale * image[span]
        for k, (src, dst) in enumerate(((sol, sol_hbm), (res, res_hbm))):
            copy = pltpu.make_async_copy(src.at[part], dst.at[part], sems.at[k, i])
            copy.start()
            copies.append(copy)
    for copy in copies:
        copy.wait()


PIECES = 2


def on_device(count, load_terms, geometry, mass_terms, element_order):
    points = load_terms.shape[0]
    cols = load_terms.shape[3]
    plane = points * points
    rows = points * plane
    deriv = gll_derivative(points)
    factors = radices(count)
    f32 = jnp.float32

    def room(*shape, dtype=f32):
        return pltpu.VMEM(shape + (cols,), dtype)

    dma = pltpu.SemaphoreType.DMA
    scratch = (
        [room(rows), room(3 * rows), room(rows), room(rows), room(rows)]
        + [
            room(2, 2 * plane), room(2, 2 * plane), room(2, 2, plane), room(2, 2, plane),
            room(2, plane), room(2, plane),
            room(2, rows - 2 * plane), room(plane), room(2, plane),
            room(2, 2, plane), room(2, 2, plane),
            room(points, dtype=jnp.int32), room(2, points, dtype=jnp.int32),
            room(2, points, dtype=jnp.int32), room(1, dtype=jnp.int32),
            room(3, points, points),
            pltpu.VMEM((len(factors), 1, 2 * cols), f32),
        ]
        + [pltpu.VMEM((w - 1, 1, 2 * cols), f32) for w in factors]
        + [
            dma((4,)), dma, dma((2,)), dma, dma((2,)), dma, dma((2,)),
            dma((2,)), dma((2, 2)), dma((len(factors),)), dma((len(factors),)),
        ]
    )
    hbm = pl.BlockSpec(memory_space=pl.ANY)
    vmem = pl.BlockSpec(memory_space=pltpu.VMEM)
    pieces = pl.pallas_call(
        functools.partial(kernel, count, points, factors, deriv),
        out_shape=(pltpu.VMEM((rows, cols), f32),) * 3 + (pltpu.VMEM((points, cols), f32),),
        in_specs=[hbm] * 4,
        out_specs=(vmem,) * 4,
        scratch_shapes=scratch,
        compiler_params=pltpu.CompilerParams(collective_id=0, has_side_effects=True),
    )(
        load_terms.reshape(rows, cols),
        geometry.reshape(3 * rows, cols),
        mass_terms.reshape(rows, cols),
        element_order,
    )
    solution_rows, residual_rows = pl.pallas_call(
        functools.partial(finish, PIECES, points),
        out_shape=(jax.ShapeDtypeStruct((rows, cols), f32),) * 2,
        in_specs=[vmem] * 4,
        out_specs=(hbm, hbm),
        scratch_shapes=[room(rows), room(rows), dma((2, PIECES))],
        compiler_params=pltpu.CompilerParams(vmem_limit_bytes=8 * rows * cols * 4),
    )(*pieces)
    shape = load_terms.shape
    return solution_rows.reshape(shape), residual_rows.reshape(shape)


def solution(mesh):
    placed = (
        P(None, None, None, "slab"),
        P(None, None, None, None, "slab"),
        P(None, None, None, "slab"),
        P("slab", None),
    )
    return jax.shard_map(
        functools.partial(on_device, mesh.shape["slab"]),
        mesh=mesh,
        in_specs=placed,
        out_specs=(P(None, None, None, "slab"), P(None, None, None, "slab")),
        check_vma=False,
    )
```

time: 22.4 us -> 20 us (0.89)
  local copies, waits for them, and re-layouts: 1.41 us -> 0 us
  Pallas kernels: 20.2 us -> 19.2 us
    pallas_call x1, Pallas kernels: 20.2 us -> 18.4 us  [on_device(): pl.pallas_call(functools.partial(kernel, count, points, factors, deriv),...]
    unnamed x2 -> x0, local copies, waits for them, and re-layouts: 1.41 us -> none
    pallas_call x0 -> x1, Pallas kernels: none -> 0.83 us  [on_device(): pl.pallas_call(functools.partial(finish, PIECES, points), out_shape=(jax....]
where the time goes in v1:
time: 20 us; the launch traced here: 19.9 us
  Pallas kernels  19.2 us (96%)
  between operations  0.64 us (3%)
    pallas_call x1, Pallas kernels, on_device(): pl.pallas_call(functools.partial(kernel, count, points, factors, deriv),...  18.4 us
    pallas_call x1, Pallas kernels, on_device(): pl.pallas_call(functools.partial(finish, PIECES, points), out_shape=(jax....  0.83 us

profile of v1, /device:TPU:0, one launch (start us, length us, event | category | flops | bytes accessed | tf_op | source)
XLA Modules:
  0.0 19.9 jit_solution(4241382311769741500)
XLA Ops:
  0.6 18.4 %shard_map.59 = (f32[512,128]{1,0:T(8,128)S(1)}, f32[512,128]{1,0:T(8,128)S(1)}, f32[512,128]{1,0:T(8,128)S(1)}, f32[8,128]{1,0:T(8,128)S(1)}) custom-call(f32[512,128]{1,0:T(8,128)} %bitcast.6, f32[1536,128]{1,0:T(8,128)} %bitcast.5, f32[512,128]{1,0:T(8,128)} %bitcast.7, s32[1,128]{1,0:T(1,128)} %order_hbm.1), custom_call_target="tpu_custom_call" | custom-call | tf_op jit(solution)/shard_map/pallas_call | solution.py:589
  19.0 0.8 %shard_map.60 = (f32[512,128]{1,0:T(8,128)}, f32[512,128]{1,0:T(8,128)}) custom-call(f32[512,128]{1,0:T(8,128)S(1)} %get-tuple-element.8.start, f32[512,128]{1,0:T(8,128)S(1)} %get-tuple-element.9.vec, f32[512,128]{1,0:T(8,128)S(1)} %get-tuple-element.10.image, f32[8,128]{1,0:T(8,128)S(1)} %get-tuple-element.11.size), custom_call_target="tpu_custom_call" | custom-call | tf_op jit(solution)/shard_map/pallas_call | solution.py:602

commit v2 on v1

--- a/solution.py
+++ b/solution.py
@@ -12,6 +12,7 @@
 EL_Z = 16
 MESH = pl.DeviceIdType.MESH
 WIDEST = 32
+HALVES = 2
 
 spectrum_centre = 1.65
 spectrum_half = 1.35
@@ -55,6 +56,10 @@
         factors.append(width)
         count //= width
     return factors
+
+
+def square_split(width):
+    return min(d for d in range(1, width + 1) if width % d == 0 and d * d >= width)
 
 
 def contract(values, table, symmetric, skip_in=0, skip_out=0):
@@ -129,7 +134,7 @@
     parts_in = rest[: len(factors)]
     (
         in_sem, first_send, first_recv, inv_send, inv_recv, pair_send, pair_recv,
-        along_send, along_recv, sum_send, sum_recv,
+        along_send, along_recv, sum_send, sum_recv, ready,
     ) = rest[len(factors):]
     me = lax.axis_index("slab")
     right = lax.rem(me + 1, count)
@@ -137,13 +142,14 @@
     plane = points * points
     rows = points * plane
     last = rows - plane
+    piece = plane // HALVES
     cols = load.shape[1]
     odd_one = lax.rem(me, 2)
     near = 1 - odd_one
     far = odd_one
     near_device = lax.rem(me + count + 1 - 2 * odd_one, count)
     far_device = lax.rem(me + count - 1 + 2 * odd_one, count)
-    device_of = ((far, far_device), (near, near_device))
+    long_way = lax.rem((me + 1) // 2, 2) == 0
 
     fetch = [
         pltpu.make_async_copy(geo_hbm, geo, in_sem.at[0]),
@@ -162,12 +168,20 @@
     barrier = pltpu.get_barrier_semaphore()
     for beside in (left, right):
         pl.semaphore_signal(barrier, inc=1, device_id=(beside,), device_id_type=MESH)
-    for stride, width in zip(strides, factors):
-        @pl.loop(1, width)
-        def _(k):
-            pl.semaphore_signal(
-                barrier, inc=1, device_id=(peer(stride, width, k),), device_id_type=MESH
-            )
+    blocks = [(stride, square_split(width)) for stride, width in zip(strides, factors)]
+    columns_of = [
+        (stride * size, width // size) for (stride, size), width in zip(blocks, factors)
+    ]
+
+    def greet(semaphore, groups):
+        for stride, width in groups:
+            @pl.loop(1, width)
+            def _(k):
+                pl.semaphore_signal(
+                    semaphore, inc=1, device_id=(peer(stride, width, k),), device_id_type=MESH
+                )
+
+    greet(barrier, blocks + columns_of)
 
     fetch[3].wait()
     cell = order[...]
@@ -305,27 +319,44 @@
         [(ends.at[s], base - plane) for s in (0, 1) for base in inner] + [(cross, 0)]
     )
 
-    def inner_to_ends():
-        for b in range(points):
-            values = [vec[at(base, b)] for base in inner]
-            for s in (0, 1):
-                inner_part[s, line(b)] = sum_of(
-                    [ends[s, at(base - plane, b)] * v for base, v in zip(inner, values)]
+    def inner_to_ends(e, b, values):
+        for s in (0, 1):
+            inner_part[e, s, line(b)] = sum_of(
+                [ends[s, at(base - plane, b)] * v for base, v in zip(inner, values)]
+            )
+
+    for b in range(points):
+        inner_to_ends(0, b, [vec[at(base, b)] for base in inner])
+
+    pl.semaphore_wait(barrier, 2 + sum(w - 1 for _, w in blocks + columns_of))
+
+    def send_first(s, device):
+        post(own_inv, near_inv.at[1 - s], inv_send, inv_recv.at[1 - s], device)
+        for h in range(HALVES):
+            for k in (0, 1):
+                part = pl.ds(k * plane + h * piece, piece)
+                post(
+                    first_out.at[s, part], first_in.at[1 - s, part], first_send,
+                    first_recv.at[1 - s, h], device,
                 )
 
-    inner_to_ends()
-
-    pl.semaphore_wait(barrier, 2 + sum(w - 1 for w in factors))
-    for s, device in device_of:
-        post(first_out.at[s], first_in.at[1 - s], first_send, first_recv.at[1 - s], device)
-        post(own_inv, near_inv.at[1 - s], inv_send, inv_recv.at[1 - s], device)
-    for s, device in device_of:
+    def send_pair(s, device):
         for k in (1, 2):
             post(
                 geo.at[pl.ds(pl.multiple_of(k * rows + s * last, points), plane)],
                 pair_in.at[1 - s, k - 1], pair_send, pair_recv.at[1 - s], device,
             )
 
+    send_first(far, far_device)
+
+    @pl.when(long_way)
+    def _():
+        send_pair(far, far_device)
+
+    send_first(near, near_device)
+    send_pair(near, near_device)
+    greet(ready, blocks)
+
     def in_plane(values, slope_geo, flux_geo):
         slopes = contract(values, deriv, False)
         fluxes = [slope_geo(b) * slopes[b] for b in range(points)]
@@ -335,7 +366,7 @@
             out[b] = out[b] + rotate_contract(flux, 1)
         return out
 
-    def apply_inner(extra):
+    def apply_inner():
         for b in range(points):
             values = [None] + [vec[at(base, b)] for base in inner] + [None]
             slopes = contract(values, deriv, False, skip_in=1)
@@ -352,20 +383,24 @@
             )
             for b in range(points):
                 span = at(base, b)
-                out = terms[b] + work[span] + mass[span] * values[b]
-                image[span] = out
-                extra(span, values[b], out)
-
-    apply_inner(lambda span, value, out: None)
+                image[span] = terms[b] + work[span] + mass[span] * values[b]
+
+    apply_inner()
     assemble_planes([(image, base) for base in inner])
 
-    def meet(s):
+    def lines_of(h):
+        return range(h * points // HALVES, (h + 1) * points // HALVES)
+
+    def meet_order(s):
         settle(near_inv.at[s], inv_send, inv_recv.at[s]).wait_recv()
-        columns = lane_gather(near_inv[s], cell8)
-        across[s] = columns
-        settle(first_in.at[s], first_send, first_recv.at[s]).wait_recv()
+        across[s] = lane_gather(near_inv[s], cell8)
+
+    def meet(s, h):
+        landed = first_in.at[s, pl.ds(0, 2 * piece)]
+        settle(landed, first_send, first_recv.at[s, h]).wait_recv()
+        columns = across[s]
         base = end_base(s)
-        for b in range(points):
+        for b in lines_of(h):
             span = at(base, b)
             begin = first_out[s, line(b)] + lane_gather(first_in[s, line(b)], columns)
             whole = first_out[s, at(plane, b)] + lane_gather(first_in[s, at(plane, b)], columns)
@@ -378,14 +413,15 @@
     def send_along(e, s, other, device):
         base = end_base(other)
         for b in range(points):
-            along_out[e, s, line(b)] = inner_part[s, line(b)] + cross[line(b)] * vec[at(base, b)]
+            along_out[e, s, line(b)] = (
+                inner_part[e, s, line(b)] + cross[line(b)] * vec[at(base, b)]
+            )
         post(
             along_out.at[e, s], along_in.at[e, 1 - s], along_send.at[e],
             along_recv.at[e, 1 - s], device,
         )
 
     def join_pair(s):
-        settle(pair_in.at[s], pair_send, pair_recv.at[s]).wait_recv()
         columns = across[s]
         for k in (0, 1):
             for b in range(points):
@@ -400,9 +436,7 @@
         values = [vec[at(base, b)] for b in range(points)]
         terms = in_plane(values, lambda b: pair[s, 0, line(b)], lambda b: pair[s, 1, line(b)])
         for b in range(points):
-            terms[b] = terms[b] - pair_diag[s, line(b)] * values[b]
-            ref[at(base, b)] = terms[b]
-        return values, terms
+            ref[at(base, b)] = terms[b] - pair_diag[s, line(b)] * values[b]
 
     def first_end(s):
         apply_end(s, image)
@@ -438,45 +472,83 @@
 
     on_load, products = [], []
 
-    def end_terms(s):
-        values, terms = apply_end(s, image)
-        for b in range(points):
-            value = values[b]
-            halved = 0.5 * value
+    def second_inner(h):
+        for b in lines_of(h):
+            values = []
+            for base in inner:
+                span = at(base, b)
+                total = add_ends(base, b)
+                value = inverse[span] * (on_start * start[span] - on_misfit * total)
+                vec[span] = value
+                values.append(value)
+            inner_to_ends(1, b, values)
+            slopes = contract([None] + values + [None], deriv, False, skip_in=1)
+            for a, slope in enumerate(slopes):
+                products.append(geo[geo_at(0, a * plane, b)] * (slope * slope))
+
+    def energy_inner():
+        for base in inner:
+            values = [vec[at(base, b)] for b in range(points)]
+            slopes = contract(values, deriv, False)
+            for b, value in enumerate(values):
+                span = at(base, b)
+                turned = rotate_contract(value, 0)
+                on_load.append(load[span] * value)
+                products.append(
+                    geo[geo_at(1, base, b)] * (slopes[b] * slopes[b])
+                    + geo[geo_at(2, base, b)] * (turned * turned)
+                    + mass[span] * (value * value)
+                )
+
+    def energy_end(s):
+        base = end_base(s)
+        values = [vec[at(base, b)] for b in range(points)]
+        slopes = contract(values, deriv, False)
+        for b, value in enumerate(values):
+            turned = rotate_contract(value, 0)
             weighted = share(b) * value
-            span = at(end_base(s), b)
-            on_load.append(0.5 * weighted * start[span])
+            on_load.append(0.5 * weighted * start[at(base, b)])
             products.append(
-                halved * terms[b]
-                + weighted * (face_diag[s, line(b)] * halved + 2.0 * inner_part[s, line(b)])
+                0.5 * (
+                    pair[s, 0, line(b)] * (slopes[b] * slopes[b])
+                    + pair[s, 1, line(b)] * (turned * turned)
+                    - pair_diag[s, line(b)] * (value * value)
+                )
+                + weighted * (0.5 * face_diag[s, line(b)] * value + 2.0 * inner_part[1, s, line(b)])
             )
 
-    meet(near)
+    meet_order(near)
+    for h in range(HALVES):
+        meet(near, h)
     send_along(0, far, near, far_device)
+
+    @pl.when(jnp.logical_not(long_way))
+    def _():
+        send_pair(far, far_device)
+
+    settle(pair_in.at[near], pair_send, pair_recv.at[near]).wait_recv()
     join_pair(near)
     first_end(near)
-    meet(far)
-    send_along(0, near, far, near_device)
-    for base in inner:
-        for b in range(points):
-            span = at(base, b)
-            total = add_ends(base, b)
-            vec[span] = inverse[span] * (on_start * start[span] - on_misfit * total)
+    meet_order(far)
+    for h in range(HALVES):
+        meet(far, h)
+        if h == HALVES - 1:
+            send_along(0, near, far, near_device)
+        second_inner(h)
+    energy_inner()
+    settle(pair_in.at[far], pair_send, pair_recv.at[far]).wait_recv()
+    pl.semaphore_wait(ready, sum(w - 1 for _, w in blocks))
     join_pair(far)
     first_end(far)
-    inner_to_ends()
-    second_end(near)
-    send_along(1, far, near, far_device)
-
-    def tally(span, value, out):
-        products.append(value * out)
-        on_load.append(load[span] * value)
-
-    apply_inner(tally)
-    end_terms(near)
-    second_end(far)
-    send_along(1, near, far, near_device)
-    end_terms(far)
+    early = jnp.where(long_way, near, far)
+    late = 1 - early
+    early_device = jnp.where(long_way, near_device, far_device)
+    late_device = jnp.where(long_way, far_device, near_device)
+    second_end(early)
+    send_along(1, late, early, late_device)
+    energy_end(early)
+    second_end(late)
+    energy_end(late)
     for b in range(points):
         products.append(
             2.0 * share(b) * cross[line(b)] * vec[at(0, b)] * vec[at(last, b)]
@@ -507,7 +579,11 @@
         return value
 
     start_sum(0, total)
-
+    send_along(1, early, late, early_device)
+
+    apply_inner()
+    for s in (near, far):
+        apply_end(s, image)
     assemble_planes([(image, base) for base in [0] + inner + [last]])
     for base in inner:
         for b in range(points):
@@ -517,7 +593,7 @@
         columns = across[s]
         for b in range(points):
             image[at(end_base(s), b)] = join_along(1, s, columns, b)
-    settle(first_out, first_send, first_recv.at[0]).wait_send()
+    settle(first_out, first_send, first_recv.at[0, 0]).wait_send()
     settle(near_inv, inv_send, inv_recv.at[0]).wait_send()
     settle(pair_in, pair_send, pair_recv.at[0]).wait_send()
     for e in (0, 1):
@@ -571,7 +647,7 @@
         + [
             room(2, 2 * plane), room(2, 2 * plane), room(2, 2, plane), room(2, 2, plane),
             room(2, plane), room(2, plane),
-            room(2, rows - 2 * plane), room(plane), room(2, plane),
+            room(2, rows - 2 * plane), room(plane), room(2, 2, plane),
             room(2, 2, plane), room(2, 2, plane),
             room(points, dtype=jnp.int32), room(2, points, dtype=jnp.int32),
             room(2, points, dtype=jnp.int32), room(1, dtype=jnp.int32),
@@ -580,8 +656,9 @@
         ]
         + [pltpu.VMEM((w - 1, 1, 2 * cols), f32) for w in factors]
         + [
-            dma((4,)), dma, dma((2,)), dma, dma((2,)), dma, dma((2,)),
+            dma((4,)), dma, dma((2, HALVES)), dma, dma((2,)), dma, dma((2,)),
             dma((2,)), dma((2, 2)), dma((len(factors),)), dma((len(factors),)),
+            pltpu.SemaphoreType.REGULAR,
         ]
     )
     hbm = pl.BlockSpec(memory_space=pl.ANY)

time: 20 us -> 18.6 us (0.930)
  Pallas kernels: 19.2 us -> 17.8 us
    pallas_call x1, Pallas kernels: 18.4 us -> 17 us  [on_device(): pl.pallas_call(functools.partial(kernel, count, points, factors, deriv),...]
where the time goes in v2:
time: 18.6 us; the launch traced here: 18.5 us
  Pallas kernels  17.8 us (96%)
  between operations  0.64 us (3%)
    pallas_call x1, Pallas kernels, on_device(): pl.pallas_call(functools.partial(kernel, count, points, factors, deriv),...  17 us
    pallas_call x1, Pallas kernels, on_device(): pl.pallas_call(functools.partial(finish, PIECES, points), out_shape=(jax....  0.83 us

profile of v2, /device:TPU:0, one launch (start us, length us, event | category | flops | bytes accessed | tf_op | source)
XLA Modules:
  0.0 18.5 jit_solution(7837707881930405744)
XLA Ops:
  0.6 17.0 %shard_map.59 = (f32[512,128]{1,0:T(8,128)S(1)}, f32[512,128]{1,0:T(8,128)S(1)}, f32[512,128]{1,0:T(8,128)S(1)}, f32[8,128]{1,0:T(8,128)S(1)}) custom-call(f32[512,128]{1,0:T(8,128)} %bitcast.6, f32[1536,128]{1,0:T(8,128)} %bitcast.5, f32[512,128]{1,0:T(8,128)} %bitcast.7, s32[1,128]{1,0:T(1,128)} %order_hbm.1), custom_call_target="tpu_custom_call" | custom-call | tf_op jit(solution)/shard_map/pallas_call | solution.py:666
  17.6 0.8 %shard_map.60 = (f32[512,128]{1,0:T(8,128)}, f32[512,128]{1,0:T(8,128)}) custom-call(f32[512,128]{1,0:T(8,128)S(1)} %get-tuple-element.8.start, f32[512,128]{1,0:T(8,128)S(1)} %get-tuple-element.9.vec, f32[512,128]{1,0:T(8,128)S(1)} %get-tuple-element.10.image, f32[8,128]{1,0:T(8,128)S(1)} %get-tuple-element.11.size), custom_call_target="tpu_custom_call" | custom-call | tf_op jit(solution)/shard_map/pallas_call | solution.py:679

commit v3 on v2

--- a/solution.py
+++ b/solution.py
@@ -129,12 +129,13 @@
     load, geo, mass, inverse, work,
     first_out, first_in, pair_in, pair, pair_diag, face_diag,
     ends, cross, inner_part, along_out, along_in,
+    relay_inv, relay_first, relay_pair, relay_along,
     own_inv, near_inv, across, order, coef, sums, *rest,
 ):
     parts_in = rest[: len(factors)]
     (
         in_sem, first_send, first_recv, inv_send, inv_recv, pair_send, pair_recv,
-        along_send, along_recv, sum_send, sum_recv, ready,
+        along_send, along_recv, sum_send, sum_recv, ready, mate_ready, relay_send, relay_recv,
     ) = rest[len(factors):]
     me = lax.axis_index("slab")
     right = lax.rem(me + 1, count)
@@ -157,31 +158,55 @@
         pltpu.make_async_copy(load_hbm, load, in_sem.at[2]),
         pltpu.make_async_copy(order_hbm, order, in_sem.at[3]),
     ]
-    for copy in fetch[::-1][:1] + fetch[:3]:
-        copy.start()
 
     def peer(stride, width, k):
         digit = lax.rem(me // stride, width)
         return me + (lax.rem(digit + k, width) - digit) * stride
 
     strides = [int(np.prod(factors[:i])) for i in range(len(factors))]
-    barrier = pltpu.get_barrier_semaphore()
-    for beside in (left, right):
-        pl.semaphore_signal(barrier, inc=1, device_id=(beside,), device_id_type=MESH)
     blocks = [(stride, square_split(width)) for stride, width in zip(strides, factors)]
     columns_of = [
         (stride * size, width // size) for (stride, size), width in zip(blocks, factors)
     ]
 
-    def greet(semaphore, groups):
-        for stride, width in groups:
+    groups = blocks + columns_of
+    relay = blocks[0][1] + 1
+    first_chip = me <= 1
+    barrier = pltpu.get_barrier_semaphore()
+
+    def signal(semaphore, device):
+        pl.semaphore_signal(semaphore, inc=1, device_id=(device,), device_id_type=MESH)
+
+    def greet(semaphore, among, wanted, beside=()):
+        for device in beside:
+            @pl.when(wanted(device))
+            def _():
+                signal(semaphore, device)
+
+        for stride, width in among:
             @pl.loop(1, width)
             def _(k):
-                pl.semaphore_signal(
-                    semaphore, inc=1, device_id=(peer(stride, width, k),), device_id_type=MESH
-                )
-
-    greet(barrier, blocks + columns_of)
+                device = peer(stride, width, k)
+
+                @pl.when(wanted(device))
+                def _():
+                    signal(semaphore, device)
+
+    @pl.when(me == count - 1)
+    def _():
+        signal(barrier, relay)
+
+    @pl.when((me == 1) | (me == relay))
+    def _():
+        signal(barrier, 0)
+
+    @pl.when(me == 0)
+    def _():
+        signal(barrier, 1)
+
+    for copy in fetch[::-1][:1] + fetch[:3]:
+        copy.start()
+    greet(barrier, groups, lambda device: device > 1, (left, right))
 
     fetch[3].wait()
     cell = order[...]
@@ -328,34 +353,71 @@
     for b in range(points):
         inner_to_ends(0, b, [vec[at(base, b)] for base in inner])
 
-    pl.semaphore_wait(barrier, 2 + sum(w - 1 for _, w in blocks + columns_of))
+    in_block = sum(w - 1 for _, w in blocks)
+    in_groups = sum(w - 1 for _, w in groups)
+    callers = jnp.where(me == 0, 2, jnp.where(me == 1, 1, 2 + in_groups))
+    pl.semaphore_wait(barrier, callers + jnp.where(me == relay, 1, 0))
+
+    def halves_of():
+        return [
+            (h, pl.ds(k * plane + h * piece, piece)) for h in range(HALVES) for k in (0, 1)
+        ]
 
     def send_first(s, device):
         post(own_inv, near_inv.at[1 - s], inv_send, inv_recv.at[1 - s], device)
-        for h in range(HALVES):
-            for k in (0, 1):
-                part = pl.ds(k * plane + h * piece, piece)
-                post(
-                    first_out.at[s, part], first_in.at[1 - s, part], first_send,
-                    first_recv.at[1 - s, h], device,
-                )
+        for h, part in halves_of():
+            post(
+                first_out.at[s, part], first_in.at[1 - s, part], first_send,
+                first_recv.at[1 - s, h], device,
+            )
+
+    def pair_source(s, k):
+        return geo.at[pl.ds(pl.multiple_of((k + 1) * rows + s * last, points), plane)]
 
     def send_pair(s, device):
-        for k in (1, 2):
+        for k in (0, 1):
             post(
-                geo.at[pl.ds(pl.multiple_of(k * rows + s * last, points), plane)],
-                pair_in.at[1 - s, k - 1], pair_send, pair_recv.at[1 - s], device,
+                pair_source(s, k), pair_in.at[1 - s, k], pair_send, pair_recv.at[1 - s], device
             )
 
-    send_first(far, far_device)
-
-    @pl.when(long_way)
-    def _():
+    @pl.when(me == 0)
+    def _():
+        post(own_inv, relay_inv, inv_send, relay_recv.at[HALVES + 2], relay)
+        for h, part in halves_of():
+            post(first_out.at[0, part], relay_first.at[part], first_send, relay_recv.at[h], relay)
+        for k in (0, 1):
+            post(pair_source(0, k), relay_pair.at[k], pair_send, relay_recv.at[HALVES], relay)
+
+    @pl.when(jnp.logical_not(first_chip))
+    def _():
+        send_first(far, far_device)
         send_pair(far, far_device)
 
     send_first(near, near_device)
     send_pair(near, near_device)
-    greet(ready, blocks)
+
+    @pl.when(jnp.logical_not(first_chip))
+    def _():
+        greet(ready, blocks, lambda device: device >= 0)
+        greet(ready, columns_of, lambda device: device <= 1, (left, right))
+
+    @pl.when(me == relay)
+    def _():
+        end = count - 1
+        settle(relay_inv, relay_send, relay_recv.at[HALVES + 2]).wait_recv()
+        post(relay_inv, near_inv.at[1], relay_send, inv_recv.at[1], end)
+        for h in range(HALVES):
+            landed = relay_first.at[pl.ds(0, 2 * piece)]
+            settle(landed, relay_send, relay_recv.at[h]).wait_recv()
+            for at_half, part in halves_of():
+                if at_half == h:
+                    post(
+                        relay_first.at[part], first_in.at[1, part], relay_send,
+                        first_recv.at[1, h], end,
+                    )
+        settle(relay_pair, relay_send, relay_recv.at[HALVES]).wait_recv()
+        for k in (0, 1):
+            post(relay_pair.at[k], pair_in.at[1, k], relay_send, pair_recv.at[1], end)
 
     def in_plane(values, slope_geo, flux_geo):
         slopes = contract(values, deriv, False)
@@ -410,16 +472,22 @@
             inverse[span] = scaled
             vec[span] = scaled * begin * (1.0 / spectrum_centre)
 
-    def send_along(e, s, other, device):
+    def put_along(e, s, other):
         base = end_base(other)
         for b in range(points):
             along_out[e, s, line(b)] = (
                 inner_part[e, s, line(b)] + cross[line(b)] * vec[at(base, b)]
             )
+
+    def post_along(e, s, device):
         post(
             along_out.at[e, s], along_in.at[e, 1 - s], along_send.at[e],
             along_recv.at[e, 1 - s], device,
         )
+
+    def send_along(e, s, other, device):
+        put_along(e, s, other)
+        post_along(e, s, device)
 
     def join_pair(s):
         columns = across[s]
@@ -520,11 +588,34 @@
     meet_order(near)
     for h in range(HALVES):
         meet(near, h)
-    send_along(0, far, near, far_device)
-
-    @pl.when(jnp.logical_not(long_way))
-    def _():
-        send_pair(far, far_device)
+    put_along(0, far, near)
+
+    @pl.when(jnp.logical_not(first_chip))
+    def _():
+        post_along(0, far, far_device)
+
+    @pl.when(me == 0)
+    def _():
+        post(
+            along_out.at[0, 0], relay_along, along_send.at[0], relay_recv.at[HALVES + 1], relay
+        )
+
+    @pl.when(me == relay)
+    def _():
+        settle(relay_along, relay_send, relay_recv.at[HALVES + 1]).wait_recv()
+        post(relay_along, along_in.at[0, 1], relay_send, along_recv.at[0, 1], count - 1)
+
+    @pl.when(first_chip)
+    def _():
+        pl.semaphore_wait(ready, in_groups)
+        greet(ready, blocks, lambda device: device > 1)
+        signal(mate_ready, 1 - me)
+
+        @pl.when(me == 1)
+        def _():
+            send_first(far, far_device)
+            post_along(0, far, far_device)
+            send_pair(far, far_device)
 
     settle(pair_in.at[near], pair_send, pair_recv.at[near]).wait_recv()
     join_pair(near)
@@ -537,7 +628,15 @@
         second_inner(h)
     energy_inner()
     settle(pair_in.at[far], pair_send, pair_recv.at[far]).wait_recv()
-    pl.semaphore_wait(ready, sum(w - 1 for _, w in blocks))
+
+    @pl.when(first_chip)
+    def _():
+        pl.semaphore_wait(mate_ready, 1)
+
+    @pl.when(jnp.logical_not(first_chip))
+    def _():
+        pl.semaphore_wait(ready, in_block)
+
     join_pair(far)
     first_end(far)
     early = jnp.where(long_way, near, far)
@@ -598,6 +697,12 @@
     settle(pair_in, pair_send, pair_recv.at[0]).wait_send()
     for e in (0, 1):
         settle(along_out.at[e], along_send.at[e], along_recv.at[0, 0]).wait_send()
+
+    @pl.when(me == relay)
+    def _():
+        for ref in (relay_inv, relay_first, relay_pair, relay_along):
+            settle(ref, relay_send, relay_recv.at[0]).wait_send()
+
     for i in range(len(factors)):
         if i:
             start_sum(i, total)
@@ -649,6 +754,7 @@
             room(2, plane), room(2, plane),
             room(2, rows - 2 * plane), room(plane), room(2, 2, plane),
             room(2, 2, plane), room(2, 2, plane),
+            room(points, dtype=jnp.int32), room(2 * plane), room(2, plane), room(plane),
             room(points, dtype=jnp.int32), room(2, points, dtype=jnp.int32),
             room(2, points, dtype=jnp.int32), room(1, dtype=jnp.int32),
             room(3, points, points),
@@ -658,7 +764,8 @@
         + [
             dma((4,)), dma, dma((2, HALVES)), dma, dma((2,)), dma, dma((2,)),
             dma((2,)), dma((2, 2)), dma((len(factors),)), dma((len(factors),)),
-            pltpu.SemaphoreType.REGULAR,
+            pltpu.SemaphoreType.REGULAR, pltpu.SemaphoreType.REGULAR,
+            dma, dma((HALVES + 3,)),
         ]
     )
     hbm = pl.BlockSpec(memory_space=pl.ANY)

time: 18.6 us -> 17.6 us (0.946)
  Pallas kernels: 17.8 us -> 16.8 us
    pallas_call x1, Pallas kernels: 17 us -> 16 us  [on_device(): pl.pallas_call(functools.partial(kernel, count, points, factors, deriv),...]
where the time goes in v3:
time: 17.6 us; the launch traced here: 17.4 us
  Pallas kernels  16.8 us (95%)
  between operations  0.64 us (4%)
    pallas_call x1, Pallas kernels, on_device(): pl.pallas_call(functools.partial(kernel, count, points, factors, deriv),...  16 us
    pallas_call x1, Pallas kernels, on_device(): pl.pallas_call(functools.partial(finish, PIECES, points), out_shape=(jax....  0.83 us

profile of v3, /device:TPU:0, one launch (start us, length us, event | category | flops | bytes accessed | tf_op | source)
XLA Modules:
  0.0 17.4 jit_solution(8064656095197995506)
XLA Ops:
  0.6 16.0 %shard_map.59 = (f32[512,128]{1,0:T(8,128)S(1)}, f32[512,128]{1,0:T(8,128)S(1)}, f32[512,128]{1,0:T(8,128)S(1)}, f32[8,128]{1,0:T(8,128)S(1)}) custom-call(f32[512,128]{1,0:T(8,128)} %bitcast.6, f32[1536,128]{1,0:T(8,128)} %bitcast.5, f32[512,128]{1,0:T(8,128)} %bitcast.7, s32[1,128]{1,0:T(1,128)} %order_hbm.1), custom_call_target="tpu_custom_call" | custom-call | tf_op jit(solution)/shard_map/pallas_call | solution.py:773
  16.6 0.8 %shard_map.60 = (f32[512,128]{1,0:T(8,128)}, f32[512,128]{1,0:T(8,128)}) custom-call(f32[512,128]{1,0:T(8,128)S(1)} %get-tuple-element.8.start, f32[512,128]{1,0:T(8,128)S(1)} %get-tuple-element.9.vec, f32[512,128]{1,0:T(8,128)S(1)} %get-tuple-element.10.image, f32[8,128]{1,0:T(8,128)S(1)} %get-tuple-element.11.size), custom_call_target="tpu_custom_call" | custom-call | tf_op jit(solution)/shard_map/pallas_call | solution.py:786

commit v4 on v3

--- a/solution.py
+++ b/solution.py
@@ -134,8 +134,8 @@
 ):
     parts_in = rest[: len(factors)]
     (
-        in_sem, first_send, first_recv, inv_send, inv_recv, pair_send, pair_recv,
-        along_send, along_recv, sum_send, sum_recv, ready, mate_ready, relay_send, relay_recv,
+        in_sem, sends, first_recv, pair_recv, along_recv, sum_send, sum_recv, ready, mate_ready,
+        relay_recv,
     ) = rest[len(factors):]
     me = lax.axis_index("slab")
     right = lax.rem(me + 1, count)
@@ -200,7 +200,7 @@
     def _():
         signal(barrier, 0)
 
-    @pl.when(me == 0)
+    @pl.when((me == 0) | (me == 2))
     def _():
         signal(barrier, 1)
 
@@ -318,6 +318,78 @@
             first_out[s, line(b)] = load[at(base, b)]
     assemble_planes([(first_out.at[s], k * plane) for s in (0, 1) for k in (0, 1)])
 
+    in_block = sum(w - 1 for _, w in blocks)
+    in_groups = sum(w - 1 for _, w in groups)
+    callers = jnp.where(me == 0, 2, jnp.where(me == 1, 2, 2 + in_groups))
+    pl.semaphore_wait(barrier, callers + jnp.where(me == relay, 1, 0))
+
+    def halves_of():
+        return [
+            (h, pl.ds(k * plane + h * piece, piece)) for h in range(HALVES) for k in (0, 1)
+        ]
+
+    def send_first(s, device):
+        post(own_inv, near_inv.at[1 - s], sends, first_recv.at[1 - s, 0], device)
+        for h, part in halves_of():
+            post(
+                first_out.at[s, part], first_in.at[1 - s, part], sends,
+                first_recv.at[1 - s, h], device,
+            )
+
+    def pair_source(s, k):
+        return geo.at[pl.ds(pl.multiple_of((k + 1) * rows + s * last, points), plane)]
+
+    def send_pair(s, device):
+        for k in (1, 0):
+            post(
+                pair_source(s, k), pair_in.at[1 - s, k], sends, pair_recv.at[1 - s, k], device
+            )
+
+    @pl.when(me == 0)
+    def _():
+        post(own_inv, relay_inv, sends, relay_recv.at[0], relay)
+        for h, part in halves_of():
+            post(first_out.at[0, part], relay_first.at[part], sends, relay_recv.at[h], relay)
+        for k in (1, 0):
+            post(pair_source(0, k), relay_pair.at[k], sends, relay_recv.at[HALVES], relay)
+
+    send_first(near, near_device)
+
+    @pl.when(jnp.logical_not((me == 0) | (me == count - 1) | (me == relay)))
+    def _():
+        send_first(far, far_device)
+        send_pair(far, far_device)
+
+    send_pair(near, near_device)
+
+    @pl.when(jnp.logical_not(first_chip))
+    def _():
+        greet(ready, blocks, lambda device: device >= 0)
+        greet(ready, columns_of, lambda device: device <= 1, (left, right))
+
+    @pl.when(me == relay)
+    def _():
+        end = count - 1
+        for h in range(HALVES):
+            landed = geo.at[pl.ds(0, 2 * piece + (0 if h else points))]
+            settle(landed, sends, relay_recv.at[h]).wait_recv()
+            if h == 0:
+                post(relay_inv, near_inv.at[1], sends, first_recv.at[1, 0], end)
+            for at_half, part in halves_of():
+                if at_half == h:
+                    post(
+                        relay_first.at[part], first_in.at[1, part], sends,
+                        first_recv.at[1, h], end,
+                    )
+        settle(relay_pair, sends, relay_recv.at[HALVES]).wait_recv()
+        for k in (1, 0):
+            post(relay_pair.at[k], pair_in.at[1, k], sends, pair_recv.at[1, k], end)
+
+    @pl.when((me == relay))
+    def _():
+        send_first(far, far_device)
+        send_pair(far, far_device)
+
     for base in inner:
         for b in range(points):
             start[at(base, b)] = load[at(base, b)]
@@ -353,71 +425,15 @@
     for b in range(points):
         inner_to_ends(0, b, [vec[at(base, b)] for base in inner])
 
-    in_block = sum(w - 1 for _, w in blocks)
-    in_groups = sum(w - 1 for _, w in groups)
-    callers = jnp.where(me == 0, 2, jnp.where(me == 1, 1, 2 + in_groups))
-    pl.semaphore_wait(barrier, callers + jnp.where(me == relay, 1, 0))
-
-    def halves_of():
-        return [
-            (h, pl.ds(k * plane + h * piece, piece)) for h in range(HALVES) for k in (0, 1)
-        ]
-
-    def send_first(s, device):
-        post(own_inv, near_inv.at[1 - s], inv_send, inv_recv.at[1 - s], device)
-        for h, part in halves_of():
-            post(
-                first_out.at[s, part], first_in.at[1 - s, part], first_send,
-                first_recv.at[1 - s, h], device,
-            )
-
-    def pair_source(s, k):
-        return geo.at[pl.ds(pl.multiple_of((k + 1) * rows + s * last, points), plane)]
-
-    def send_pair(s, device):
-        for k in (0, 1):
-            post(
-                pair_source(s, k), pair_in.at[1 - s, k], pair_send, pair_recv.at[1 - s], device
-            )
-
-    @pl.when(me == 0)
-    def _():
-        post(own_inv, relay_inv, inv_send, relay_recv.at[HALVES + 2], relay)
-        for h, part in halves_of():
-            post(first_out.at[0, part], relay_first.at[part], first_send, relay_recv.at[h], relay)
-        for k in (0, 1):
-            post(pair_source(0, k), relay_pair.at[k], pair_send, relay_recv.at[HALVES], relay)
-
-    @pl.when(jnp.logical_not(first_chip))
+    @pl.when(me == count - 1)
     def _():
         send_first(far, far_device)
         send_pair(far, far_device)
 
-    send_first(near, near_device)
-    send_pair(near, near_device)
-
-    @pl.when(jnp.logical_not(first_chip))
-    def _():
-        greet(ready, blocks, lambda device: device >= 0)
-        greet(ready, columns_of, lambda device: device <= 1, (left, right))
-
     @pl.when(me == relay)
     def _():
-        end = count - 1
-        settle(relay_inv, relay_send, relay_recv.at[HALVES + 2]).wait_recv()
-        post(relay_inv, near_inv.at[1], relay_send, inv_recv.at[1], end)
-        for h in range(HALVES):
-            landed = relay_first.at[pl.ds(0, 2 * piece)]
-            settle(landed, relay_send, relay_recv.at[h]).wait_recv()
-            for at_half, part in halves_of():
-                if at_half == h:
-                    post(
-                        relay_first.at[part], first_in.at[1, part], relay_send,
-                        first_recv.at[1, h], end,
-                    )
-        settle(relay_pair, relay_send, relay_recv.at[HALVES]).wait_recv()
-        for k in (0, 1):
-            post(relay_pair.at[k], pair_in.at[1, k], relay_send, pair_recv.at[1], end)
+        settle(relay_along, sends, relay_recv.at[HALVES + 1]).wait_recv()
+        post(relay_along, along_in.at[0, 1], sends, along_recv.at[0, 1], count - 1)
 
     def in_plane(values, slope_geo, flux_geo):
         slopes = contract(values, deriv, False)
@@ -453,13 +469,11 @@
     def lines_of(h):
         return range(h * points // HALVES, (h + 1) * points // HALVES)
 
-    def meet_order(s):
-        settle(near_inv.at[s], inv_send, inv_recv.at[s]).wait_recv()
-        across[s] = lane_gather(near_inv[s], cell8)
-
     def meet(s, h):
-        landed = first_in.at[s, pl.ds(0, 2 * piece)]
-        settle(landed, first_send, first_recv.at[s, h]).wait_recv()
+        landed = geo.at[pl.ds(0, 2 * piece + (0 if h else points))]
+        settle(landed, sends, first_recv.at[s, h]).wait_recv()
+        if h == 0:
+            across[s] = lane_gather(near_inv[s], cell8)
         columns = across[s]
         base = end_base(s)
         for b in lines_of(h):
@@ -481,7 +495,7 @@
 
     def post_along(e, s, device):
         post(
-            along_out.at[e, s], along_in.at[e, 1 - s], along_send.at[e],
+            along_out.at[e, s], along_in.at[e, 1 - s], sends,
             along_recv.at[e, 1 - s], device,
         )
 
@@ -489,15 +503,35 @@
         put_along(e, s, other)
         post_along(e, s, device)
 
-    def join_pair(s):
+    def join_pair(s, k):
+        settle(pair_in.at[s, k], sends, pair_recv.at[s, k]).wait_recv()
         columns = across[s]
-        for k in (0, 1):
-            for b in range(points):
-                own = geo[geo_at(k + 1, s * last, b)]
-                pair[s, k, line(b)] = own + lane_gather(pair_in[s, k, line(b)], columns)
-        terms = contract([pair[s, 0, line(b)] for b in range(points)], square.T, True)
-        for b in range(points):
-            pair_diag[s, line(b)] = terms[b] + rotate_contract(pair[s, 1, line(b)], 2)
+        for b in range(points):
+            own = geo[geo_at(k + 1, s * last, b)]
+            pair[s, k, line(b)] = own + lane_gather(pair_in[s, k, line(b)], columns)
+
+    def first_third(s):
+        join_pair(s, 1)
+        for b in range(points):
+            span = at(end_base(s), b)
+            both = pair[s, 1, line(b)]
+            value = vec[span]
+            own = rotate_contract(both, 2)
+            pair_diag[s, line(b)] = own
+            image[span] = rotate_contract(both * rotate_contract(value, 0), 1) - own * value
+
+    def first_second(s):
+        join_pair(s, 0)
+        both = [pair[s, 0, line(b)] for b in range(points)]
+        values = [vec[at(end_base(s), b)] for b in range(points)]
+        own = contract(both, square.T, True)
+        slopes = contract(values, deriv, False)
+        terms = contract([g * slope for g, slope in zip(both, slopes)], deriv.T, False)
+        for b in range(points):
+            span = at(end_base(s), b)
+            pair_diag[s, line(b)] = pair_diag[s, line(b)] + own[b]
+            image[span] = image[span] + terms[b] - own[b] * values[b]
+        assemble_planes([(image, end_base(s))])
 
     def apply_end(s, ref):
         base = end_base(s)
@@ -505,10 +539,6 @@
         terms = in_plane(values, lambda b: pair[s, 0, line(b)], lambda b: pair[s, 1, line(b)])
         for b in range(points):
             ref[at(base, b)] = terms[b] - pair_diag[s, line(b)] * values[b]
-
-    def first_end(s):
-        apply_end(s, image)
-        assemble_planes([(image, end_base(s))])
 
     ratio_sigma = spectrum_centre / spectrum_half
     rho_prev = 1.0 / ratio_sigma
@@ -531,7 +561,7 @@
         )
 
     def second_end(s):
-        settle(along_in.at[0, s], along_send.at[0], along_recv.at[0, s]).wait_recv()
+        settle(along_in.at[0, s], sends, along_recv.at[0, s]).wait_recv()
         columns = across[s]
         for b in range(points):
             span = at(end_base(s), b)
@@ -553,20 +583,19 @@
             slopes = contract([None] + values + [None], deriv, False, skip_in=1)
             for a, slope in enumerate(slopes):
                 products.append(geo[geo_at(0, a * plane, b)] * (slope * slope))
-
-    def energy_inner():
-        for base in inner:
-            values = [vec[at(base, b)] for b in range(points)]
-            slopes = contract(values, deriv, False)
-            for b, value in enumerate(values):
+            for base, value in zip(inner, values):
                 span = at(base, b)
                 turned = rotate_contract(value, 0)
                 on_load.append(load[span] * value)
                 products.append(
-                    geo[geo_at(1, base, b)] * (slopes[b] * slopes[b])
-                    + geo[geo_at(2, base, b)] * (turned * turned)
-                    + mass[span] * (value * value)
+                    geo[geo_at(2, base, b)] * (turned * turned) + mass[span] * (value * value)
                 )
+
+    def energy_inner():
+        for base in inner:
+            slopes = contract([vec[at(base, b)] for b in range(points)], deriv, False)
+            for b, slope in enumerate(slopes):
+                products.append(geo[geo_at(1, base, b)] * (slope * slope))
 
     def energy_end(s):
         base = end_base(s)
@@ -585,25 +614,19 @@
                 + weighted * (0.5 * face_diag[s, line(b)] * value + 2.0 * inner_part[1, s, line(b)])
             )
 
-    meet_order(near)
     for h in range(HALVES):
         meet(near, h)
     put_along(0, far, near)
 
-    @pl.when(jnp.logical_not(first_chip))
+    @pl.when(me > 0)
     def _():
         post_along(0, far, far_device)
 
     @pl.when(me == 0)
     def _():
         post(
-            along_out.at[0, 0], relay_along, along_send.at[0], relay_recv.at[HALVES + 1], relay
+            along_out.at[0, 0], relay_along, sends, relay_recv.at[HALVES + 1], relay
         )
-
-    @pl.when(me == relay)
-    def _():
-        settle(relay_along, relay_send, relay_recv.at[HALVES + 1]).wait_recv()
-        post(relay_along, along_in.at[0, 1], relay_send, along_recv.at[0, 1], count - 1)
 
     @pl.when(first_chip)
     def _():
@@ -611,23 +634,14 @@
         greet(ready, blocks, lambda device: device > 1)
         signal(mate_ready, 1 - me)
 
-        @pl.when(me == 1)
-        def _():
-            send_first(far, far_device)
-            post_along(0, far, far_device)
-            send_pair(far, far_device)
-
-    settle(pair_in.at[near], pair_send, pair_recv.at[near]).wait_recv()
-    join_pair(near)
-    first_end(near)
-    meet_order(far)
+    first_third(near)
+    first_second(near)
     for h in range(HALVES):
         meet(far, h)
         if h == HALVES - 1:
             send_along(0, near, far, near_device)
         second_inner(h)
     energy_inner()
-    settle(pair_in.at[far], pair_send, pair_recv.at[far]).wait_recv()
 
     @pl.when(first_chip)
     def _():
@@ -637,8 +651,12 @@
     def _():
         pl.semaphore_wait(ready, in_block)
 
-    join_pair(far)
-    first_end(far)
+    first_third(far)
+
+    @pl.when(jnp.logical_not(long_way))
+    def _():
+        first_second(far)
+
     early = jnp.where(long_way, near, far)
     late = 1 - early
     early_device = jnp.where(long_way, near_device, far_device)
@@ -646,6 +664,13 @@
     second_end(early)
     send_along(1, late, early, late_device)
     energy_end(early)
+    on_load[:] = [sum_of(on_load)]
+    products[:] = [sum_of(products)]
+
+    @pl.when(long_way)
+    def _():
+        first_second(far)
+
     second_end(late)
     energy_end(late)
     for b in range(points):
@@ -667,15 +692,17 @@
     def start_sum(i, value):
         sums[i] = value
 
-        @pl.loop(1, factors[i])
-        def _(k):
-            sum_copy(i, k).start()
+        width = factors[i]
+        digit = lax.rem(me // strides[i], width)
+
+        @pl.loop(0, width - 1)
+        def _(j):
+            target = j + jnp.where(j >= digit, 1, 0)
+            sum_copy(i, lax.rem(target - digit + width, width)).start()
 
     def finish_sum(i, value):
         settle(parts_in[i], sum_send.at[i], sum_recv.at[i]).wait()
-        for k in range(factors[i] - 1):
-            value = value + parts_in[i][k]
-        return value
+        return sum_of([value] + [parts_in[i][k] for k in range(factors[i] - 1)])
 
     start_sum(0, total)
     send_along(1, early, late, early_device)
@@ -688,20 +715,20 @@
         for b in range(points):
             image[at(base, b)] = add_ends(base, b)
     for s in (near, far):
-        settle(along_in.at[1, s], along_send.at[1], along_recv.at[1, s]).wait_recv()
+        settle(along_in.at[1, s], sends, along_recv.at[1, s]).wait_recv()
         columns = across[s]
         for b in range(points):
             image[at(end_base(s), b)] = join_along(1, s, columns, b)
-    settle(first_out, first_send, first_recv.at[0, 0]).wait_send()
-    settle(near_inv, inv_send, inv_recv.at[0]).wait_send()
-    settle(pair_in, pair_send, pair_recv.at[0]).wait_send()
-    for e in (0, 1):
-        settle(along_out.at[e], along_send.at[e], along_recv.at[0, 0]).wait_send()
+    sent = 12 * plane + 2 * points
+    passed_on = 5 * plane + points
 
     @pl.when(me == relay)
     def _():
-        for ref in (relay_inv, relay_first, relay_pair, relay_along):
-            settle(ref, relay_send, relay_recv.at[0]).wait_send()
+        settle(geo.at[pl.ds(0, sent + passed_on)], sends, first_recv.at[0, 0]).wait_send()
+
+    @pl.when(me != relay)
+    def _():
+        settle(geo.at[pl.ds(0, sent)], sends, first_recv.at[0, 0]).wait_send()
 
     for i in range(len(factors)):
         if i:
@@ -762,10 +789,9 @@
         ]
         + [pltpu.VMEM((w - 1, 1, 2 * cols), f32) for w in factors]
         + [
-            dma((4,)), dma, dma((2, HALVES)), dma, dma((2,)), dma, dma((2,)),
-            dma((2,)), dma((2, 2)), dma((len(factors),)), dma((len(factors),)),
-            pltpu.SemaphoreType.REGULAR, pltpu.SemaphoreType.REGULAR,
-            dma, dma((HALVES + 3,)),
+            dma((4,)), dma, dma((2, HALVES)), dma((2, 2)), dma((2, 2)),
+            dma((len(factors),)), dma((len(factors),)),
+            pltpu.SemaphoreType.REGULAR, pltpu.SemaphoreType.REGULAR, dma((HALVES + 2,)),
         ]
     )
     hbm = pl.BlockSpec(memory_space=pl.ANY)

time: 17.6 us -> 17.5 us (level)
  no operation moved by 1% of the time
where the time goes in v4:
time: 17.5 us; the launch traced here: 17.3 us
  Pallas kernels  16.7 us (95%)
  between operations  0.64 us (4%)
    pallas_call x1, Pallas kernels, on_device(): pl.pallas_call(functools.partial(kernel, count, points, factors, deriv),...  15.9 us
    pallas_call x1, Pallas kernels, on_device(): pl.pallas_call(functools.partial(finish, PIECES, points), out_shape=(jax....  0.83 us

profile of v4, /device:TPU:0, one launch (start us, length us, event | category | flops | bytes accessed | tf_op | source)
XLA Modules:
  0.0 17.3 jit_solution(17475283820437105820)
XLA Ops:
  0.6 15.9 %shard_map.59 = (f32[512,128]{1,0:T(8,128)S(1)}, f32[512,128]{1,0:T(8,128)S(1)}, f32[512,128]{1,0:T(8,128)S(1)}, f32[8,128]{1,0:T(8,128)S(1)}) custom-call(f32[512,128]{1,0:T(8,128)} %bitcast.6, f32[1536,128]{1,0:T(8,128)} %bitcast.5, f32[512,128]{1,0:T(8,128)} %bitcast.7, s32[1,128]{1,0:T(1,128)} %order_hbm.1), custom_call_target="tpu_custom_call" | custom-call | tf_op jit(solution)/shard_map/pallas_call | solution.py:799
  16.5 0.8 %shard_map.60 = (f32[512,128]{1,0:T(8,128)}, f32[512,128]{1,0:T(8,128)}) custom-call(f32[512,128]{1,0:T(8,128)S(1)} %get-tuple-element.8.start, f32[512,128]{1,0:T(8,128)S(1)} %get-tuple-element.9.vec, f32[512,128]{1,0:T(8,128)S(1)} %get-tuple-element.10.image, f32[8,128]{1,0:T(8,128)S(1)} %get-tuple-element.11.size), custom_call_target="tpu_custom_call" | custom-call | tf_op jit(solution)/shard_map/pallas_call | solution.py:812
